TPU v7x, 256 devices: a whole 4x4x8 slice. The times are simulated.
256 devices in a mesh: seq: 8 (over x, core), dom: 32 (over z, y).
Axes of the slice: x: 4, y: 4, z: 8, core: 2. Of those that a mesh axis runs over, the one named last changes fastest.
Arguments:
- observed: bfloat16 [40, 88], P('seq'), parts along dimension 0, may hold values from -18 to 18
- latent_noise: float32 [4, 128, 32768], P(None, None, ('seq', 'dom')), parts along dimension 2, may hold values from -6 to 6
- w_hidden: bfloat16 [4096, 1024], replicated, may hold values from -0.1875 to 0.1875
- w_latent: bfloat16 [4096, 128], replicated, may hold values from -0.5 to 0.5
- w_frame: bfloat16 [88, 4096], replicated, may hold values from -0.625 to 0.625
- gate_bias: float32 [4096], replicated, may hold values from -3 to 3
- w_prior: bfloat16 [256, 1024], replicated, may hold values from -0.1875 to 0.1875
- w_emit: bfloat16 [88, 128], replicated, may hold values from -0.09375 to 0.09375
- w_emit_hidden: bfloat16 [88, 1024], replicated, may hold values from -0.046875 to 0.046875
- block_source: int32 [24, 32], P('seq'), parts along dimension 0, may hold values from 0 to 31, as said below
- inner_offset: int32 [24, 4096], P('seq'), parts along dimension 0, may hold values from 0 to 127
- resample_flags: int32 [3], replicated, may hold values from 0 to 1, as said below
Outputs:
- final_hidden: bfloat16 [1024, 32768], P(None, ('seq', 'dom')), parts along dimension 1
- fivo_bound: float32 [8], P('seq'), parts along dimension 0
There are 8 independent parts, one for each index of `seq`. A program takes and returns all parts, laid end to end along the dimension named above; an argument that names none is the same for every part. Nothing has to cross between parts.
Inputs may be any that keep to these rules, and one draw needn't show every extreme that they name: block_source[t, j] differs from j by at most 1 for every transition t and block j; in every draw some block takes the particles of the block 1 places before it and some those of the block 1 places after it. `resample_flags`: at least one entry is 1 and at least one is 0.
All inputs are finite; a program needn't handle non-finite values.
Results may differ from a plain program's by a relative error of at most 0.0023.
The roundings to bfloat16 on the way count: a program that leaves them out, or rounds other values in their place, can miss the bound.
Values may be sent and summed in bfloat16 or wider, within the bound.
A program may use at most 64 MiB of HBM per device.

v0:
```python
import functools
import math

import jax
import jax.numpy as jnp
from jax import lax
from jax.experimental import pallas as pl
from jax.experimental.pallas import tpu as pltpu
from jax.sharding import PartitionSpec as P

BLK = 128
F32 = jnp.float32
BF16 = jnp.bfloat16
MESH = pl.DeviceIdType.MESH
CH = 4


def mm(a, b):
    return jnp.dot(a, b, preferred_element_type=F32)


def sig(x):
    return 0.5 * jnp.tanh(0.5 * x) + 0.5


def cell_update(gates, old, n):
    in_gate = sig(gates[:n])
    forget = sig(gates[n : 2 * n])
    cand = jnp.tanh(gates[2 * n : 3 * n])
    out_gate = sig(gates[3 * n :])
    fresh = forget * old.astype(F32) + in_gate * cand
    return (out_gate * jnp.tanh(fresh)).astype(BF16), fresh.astype(BF16)


def split3(x):
    hi = x.astype(BF16)
    rest = x - hi.astype(F32)
    mid = rest.astype(BF16)
    return hi, mid, (rest - mid.astype(F32)).astype(BF16)


def kernel(
    D,
    obs_h,
    nz_h,
    wh_h,
    wl_h,
    wf_h,
    bias_h,
    wp_h,
    we_h,
    weh_h,
    bs_h,
    off_h,
    fl_h,
    hid_o,
    bnd_o,
    wh,
    wlf,
    wf,
    tpose,
    bias,
    wp,
    we,
    weh,
    obs,
    obs_pad,
    nz,
    off,
    bs,
    fl,
    from_l,
    from_r,
    x0,
    x0_l,
    x0_r,
    x1,
    x1_l,
    x1_r,
    g1,
    ga,
    gb,
    hz,
    cz,
    h1,
    c1,
    hc,
    cc,
    h2,
    c2,
    h3,
    c3,
    h4,
    lse_row,
    lse_all,
    wsem,
    lsem,
    osem,
    ssem,
    rsem,
    as_sem,
    ar_sem,
    near_sem,
):
    H = wh.shape[2]
    Z = we.shape[1]
    X = we.shape[0]
    HC = H // CH
    me = lax.axis_index("dom")
    right = lax.rem(me + 1, D)
    left = lax.rem(me + D - 1, D)

    barrier = pltpu.get_barrier_semaphore()
    for nb in (left, right):
        pl.semaphore_signal(barrier, inc=1, device_id={"dom": nb}, device_id_type=MESH)

    small = []

    def fetch(src, dst):
        cp = pltpu.make_async_copy(src, dst, lsem.at[len(small)])
        cp.start()
        small.append(cp)
        return cp

    cp_nz = [fetch(nz_h.at[t], nz.at[t]) for t in range(2)]
    cp_bs = fetch(bs_h, bs)
    cp_fl = fetch(fl_h, fl)
    cp_wf = fetch(wf_h, wf)
    cp_bias = fetch(bias_h, bias)
    cp_obs = fetch(obs_h, obs)
    cp_off = fetch(off_h, off)

    def weight_copies(c):
        res = []
        for g in range(4):
            rows = pl.ds(g * H + c * HC, HC)
            res.append(
                pltpu.make_async_copy(
                    wh_h.at[rows, :], wh.at[c, pl.ds(g * HC, HC), :], wsem.at[0, c, g]
                )
            )
            res.append(
                pltpu.make_async_copy(
                    wl_h.at[rows, :], wlf.at[c, pl.ds(g * HC, HC), pl.ds(0, Z)], wsem.at[1, c, g]
                )
            )
        return res

    wcp = [weight_copies(c) for c in range(CH)]
    for cp in wcp[0]:
        cp.start()
    cp_wp = fetch(wp_h, wp)
    cp_nz += [fetch(nz_h.at[t], nz.at[t]) for t in range(2, 4)]
    cp_we = fetch(we_h, we)
    cp_weh = fetch(weh_h, weh)
    for c in range(1, CH):
        for cp in wcp[c]:
            cp.start()

    def send(k, src, to_right_dst, to_left_dst):
        res = []
        for side, (dst, dev) in enumerate(((to_right_dst, right), (to_left_dst, left))):
            cp = pltpu.make_async_remote_copy(
                src_ref=src,
                dst_ref=dst,
                send_sem=ssem.at[side, k],
                recv_sem=rsem.at[side, k],
                device_id={"dom": dev},
                device_id_type=MESH,
            )
            cp.start()
            res.append(cp)
        return res

    hz[...] = jnp.zeros_like(hz)
    cz[...] = jnp.zeros_like(cz)
    obs_pad[...] = jnp.zeros_like(obs_pad)
    tpose[X // 16 * 16 :, :] = jnp.zeros((BLK - X // 16 * 16, tpose.shape[1]), BF16)

    cp_nz[0].wait()
    cp_nz[1].wait()
    pl.semaphore_wait(barrier, 2)
    sent = []
    for t in range(2):
        sent += [send(t, nz.at[t], from_l.at[t], from_r.at[t])]

    cp_bs.wait()
    cp_fl.wait()
    cp_off.wait()
    cp_obs.wait()
    f0, f1, f2 = fl[0] == 1, fl[1] == 1, fl[2] == 1

    around = range(-2, 3)
    place = [lax.rem(me + d + D, D) for d in around]

    def src(t, k, f):
        found = bs[t, place[2]]
        for d, p in zip(around, place):
            found = jnp.where(k - me == d, bs[t, p], found)
        return jnp.where(f, found, k)

    lane = lax.broadcasted_iota(jnp.int32, (1, BLK), 1).astype(F32)
    sub_i = lax.broadcasted_iota(jnp.int32, (BLK, BLK), 0)
    sub = sub_i.astype(F32)

    def flag_mask(f, shape):
        return jnp.broadcast_to(f.astype(jnp.int32), shape) > 0

    def offs(t, k, f):
        away = jnp.broadcast_to(k - me, (1, BLK))
        row = lane
        for d, p in zip(around, place):
            there = off[pl.ds(t, 1), pl.ds(pl.multiple_of(p * BLK, BLK), BLK)].astype(F32)
            row = jnp.where(jnp.logical_and(flag_mask(f, (1, BLK)), away == d), there, row)
        return row

    def onehot(row):
        return jnp.where(sub == row, 1.0, 0.0).astype(BF16)

    def comp(row, hot):
        return mm(jnp.broadcast_to(row, (16, BLK)).astype(BF16), hot)[:1]

    k2 = src(2, me, f2)
    k1 = src(1, k2, f1)
    s1 = src(1, me, f1)
    s0 = src(0, me, f0)
    both = jnp.logical_and(f0, f1)
    hot_q = onehot(offs(2, me, f2))
    hot_r = onehot(comp(offs(1, k2, f1), hot_q))
    hot_s = onehot(comp(offs(0, k1, f0), hot_r))
    hot_o1 = onehot(offs(1, me, f1))
    hot_o0 = onehot(comp(offs(0, s1, f0), hot_o1))
    hot_c0 = onehot(offs(0, me, f0))
    x0_src = jnp.where(f0, s0, s1)
    hop_o = jnp.where(both, s1, me)
    hop_l = jnp.where(f2, k2, hop_o)

    def pick(a, b, c, k):
        d = jnp.broadcast_to(k - me, a.shape)
        return jnp.where(d < 0, a, jnp.where(d > 0, c, b))

    def gather3(x, hot):
        hi, mid, lo = split3(x)
        out = mm(jnp.concatenate([hi, mid, lo], axis=0), hot)
        return out[:BLK] + out[BLK : 2 * BLK] + out[2 * BLK :]

    steps = obs.shape[0] - 1
    obs_pad[0 : steps + 1, 0:X] = obs[...].astype(F32)
    obs_t = jnp.transpose(obs_pad[...])

    def frame_col(t):
        return jnp.broadcast_to(obs_t[:, t : t + 1], (BLK, BLK))

    ones = jnp.logical_and(sub_i >= 96, sub_i < 99)
    tails = [jnp.where(ones, 1.0, frame_col(t)).astype(BF16) for t in range(steps)]

    cp_wf.wait()
    cp_bias.wait()
    tpose[0:X, :] = wf[...]
    hi, mid, lo = (p.astype(F32) for p in split3(bias[...]))
    r16 = lax.broadcasted_iota(jnp.int32, (16, bias.shape[1]), 0)
    tpose[96:112, :] = jnp.where(
        r16 == 0, hi, jnp.where(r16 == 1, mid, jnp.where(r16 == 2, lo, 0.0))
    ).astype(BF16)
    for c in range(CH):
        for g in range(4):
            for i in range(0, HC, BLK):
                rows = g * H + c * HC + i
                wlf[c, g * HC + i : g * HC + i + BLK, Z : Z + BLK] = jnp.transpose(
                    tpose[:, rows : rows + BLK]
                )

    def run_layer(gates, elem):
        bufs = (ga, gb)
        for c in range(CH):
            val = gates(c)
            bufs[c % 2][:, : val.shape[1]] = val
            if c:
                elem(c - 1, bufs[(c - 1) % 2])
        elem(CH - 1, bufs[(CH - 1) % 2])

    def elem_of(n, old, h_out, c_out):
        def elem(c, buf):
            rows = slice(c * HC, (c + 1) * HC)
            h, s = cell_update(buf[:, :n], old[rows, :n], HC)
            h_out[rows, :n] = h
            if c_out is not None:
                c_out[rows, :n] = s

        return elem

    def moments(h):
        p = mm(wp[...], h)
        return p[:Z], jnp.exp(0.5 * jnp.tanh(p[Z:]))

    def increment(t, lat, h):
        pred = mm(we[...], lat) + mm(weh[...], h)
        target = frame_col(t + 1)[:X]
        return jnp.sum(pred * (target - 0.5 * pred), axis=0, keepdims=True)

    lat_tail0 = jnp.concatenate([jnp.zeros((Z, BLK), BF16), tails[0]], axis=0)

    def gates0(c):
        for cp in wcp[c]:
            cp.wait()
        return mm(wh[c], hz[...]) + mm(wlf[c], lat_tail0)

    run_layer(gates0, elem_of(BLK, cz, h1, c1))
    cp_wp.wait()
    mean0, std0 = moments(h1[...])
    cp_we.wait()
    cp_weh.wait()
    lw0 = increment(0, (mean0 + std0 * nz[0]).astype(BF16), h1[...])

    for c in range(CH // 2):
        g1[c] = mm(wh[c], h1[...])

    def near(i, dist):
        for dev in (lax.rem(me + dist, D), lax.rem(me + D - dist, D)):
            pl.semaphore_signal(
                near_sem.at[i], inc=1, device_id={"dom": dev}, device_id_type=MESH
            )

    near(0, 1)

    def arrived(k, bufs):
        for cp in bufs[k]:
            cp.wait_recv()

    arrived(0, sent)
    n0 = pick(from_l[0], nz[0], from_r[0], x0_src)
    x0[...] = (mean0 + std0 * n0).astype(BF16)
    arrived(1, sent)
    x1[...] = pick(from_l[1], nz[1], from_r[1], s1)
    for c in range(CH // 2, CH):
        g1[c] = mm(wh[c], h1[...])
    sent += [send(2, x0, x0_l, x0_r)]
    sent += [send(3, x1, x1_l, x1_r)]
    cp_nz[2].wait()
    cp_nz[3].wait()
    sent += [send(4, nz.at[2], from_l.at[2], from_r.at[2])]
    pl.semaphore_wait(near_sem.at[0], 2)
    dist, count = 2, 1
    waits = []
    while dist < D // 2:
        waits.append((count, dist))
        dist, count = dist * 2, count + 1

    lat_c = mm(
        (mean0 + std0 * pick(from_l[0], nz[0], from_r[0], s0)).astype(BF16), hot_c0
    ).astype(BF16)
    tail_c = jnp.concatenate([lat_c, tails[1]], axis=0)
    run_layer(lambda c: g1[c] + mm(wlf[c], tail_c), elem_of(BLK, c1, hc, None))
    mean_c, std_c = moments(hc[...])
    inc_c = increment(1, (mean_c + std_c * nz[1]).astype(BF16), hc[...])
    lw1 = jnp.where(flag_mask(f0, (1, BLK)), 0.0, lw0) + inc_c

    for i, d in waits[:1]:
        near(i, d)
    arrived(2, sent)
    x0s = (x0_l[...].astype(F32), x0[...].astype(F32), x0_r[...].astype(F32))
    lat_o = mm(pick(*x0s, hop_o).astype(BF16), hot_o0).astype(BF16)
    lat_l = mm(pick(*x0s, hop_l).astype(BF16), hot_s).astype(BF16)
    tail_ol = jnp.concatenate(
        [
            jnp.concatenate([lat_o, lat_l], axis=1),
            jnp.concatenate([tails[1], tails[1]], axis=1),
        ],
        axis=0,
    )

    def gates1(c):
        g = g1[c]
        return jnp.concatenate([g, g], axis=1) + mm(wlf[c], tail_ol)

    def elem1(c, buf):
        rows = slice(c * HC, (c + 1) * HC)
        old = c1[rows, :]
        h, s = cell_update(buf[...], jnp.concatenate([old, old], axis=1), HC)
        h2[rows, :] = h
        c2[rows, :] = s

    run_layer(gates1, elem1)
    for i, d in waits[:1]:
        pl.semaphore_wait(near_sem.at[i], 2)
    for i, d in waits[1:2]:
        near(i, d)
    m1, sd1 = moments(h2[...])
    arrived(3, sent)
    n1_o = gather3(x1[...], hot_o1)
    n1_l = gather3(pick(x1_l[...], x1[...], x1_r[...], k2), hot_r)
    lat1 = (m1 + sd1 * jnp.concatenate([n1_o, n1_l], axis=1)).astype(BF16)

    tail2 = jnp.concatenate(
        [lat1, jnp.concatenate([tails[2], tails[2]], axis=1)], axis=0
    )
    run_layer(
        lambda c: mm(wh[c], h2[...]) + mm(wlf[c], tail2), elem_of(2 * BLK, c2, h3, c3)
    )
    for i, d in waits[1:2]:
        pl.semaphore_wait(near_sem.at[i], 2)
    for i, d in waits[2:3]:
        near(i, d)
    m2, sd2 = moments(h3[...])
    arrived(4, sent)
    n2_l = gather3(pick(from_l[2], nz[2], from_r[2], k2), hot_q)
    lat2 = (m2 + sd2 * jnp.concatenate([nz[2], n2_l], axis=1)).astype(BF16)
    inc2 = increment(2, lat2[:, :BLK], h3[:, :BLK])
    lw2 = jnp.where(flag_mask(f1, (1, BLK)), 0.0, lw1) + inc2

    tail3 = jnp.concatenate([lat2[:, BLK:], tails[3]], axis=0)

    def gates3(c):
        return mm(wh[c], h3[:, BLK:]) + mm(wlf[c], tail3)

    def elem3(c, buf):
        rows = slice(c * HC, (c + 1) * HC)
        h, _ = cell_update(buf[:, :BLK], c3[rows, BLK:], HC)
        h4[rows, :] = h

    run_layer(gates3, elem3)
    out_cp = pltpu.make_async_copy(h4, hid_o, osem)
    out_cp.start()
    for i, d in waits[2:3]:
        pl.semaphore_wait(near_sem.at[i], 2)
    m3, sd3 = moments(h4[...])
    lat3 = (m3 + sd3 * nz[3]).astype(BF16)
    lw3 = jnp.where(flag_mask(f2, (1, BLK)), 0.0, lw2) + increment(3, lat3, h4[...])

    def lse(lw):
        peak = jnp.max(lw, axis=1, keepdims=True)
        return peak + jnp.log(jnp.sum(jnp.exp(lw - peak), axis=1, keepdims=True))

    lane_i = lax.broadcasted_iota(jnp.int32, (1, BLK), 1)
    row = jnp.zeros((1, BLK), F32)
    for t, lw in enumerate((lw0, lw1, lw2, lw3)):
        row = jnp.where(lane_i == t, lse(lw), row)
    lse_row[...] = row
    lse_all[pl.ds(me, 1)] = row[None]
    pushes = []
    for d in range(1, D):
        dev = lax.rem(me + d, D)
        cp = pltpu.make_async_remote_copy(
            src_ref=lse_row,
            dst_ref=lse_all.at[me],
            send_sem=as_sem.at[d],
            recv_sem=ar_sem.at[me],
            device_id={"dom": dev},
            device_id_type=MESH,
        )
        cp.start()
        pushes.append(cp)
    for two in sent:
        for cp in two:
            cp.wait_send()
    out_cp.wait()
    for d in range(1, D):
        frm = lax.rem(me + d, D)
        pltpu.make_async_remote_copy(
            src_ref=lse_row,
            dst_ref=lse_all.at[frm],
            send_sem=as_sem.at[d],
            recv_sem=ar_sem.at[frm],
            device_id={"dom": frm},
            device_id_type=MESH,
        ).wait_recv()
    for cp in pushes:
        cp.wait_send()
    every = lse_all[...]
    peak = jnp.max(every, axis=0)
    level = peak + jnp.log(jnp.sum(jnp.exp(every - peak[None]), axis=0)) - math.log(D * BLK)
    used = lane_i == steps - 1
    for t, f in enumerate((f0, f1, f2)):
        used = jnp.logical_or(used, jnp.logical_and(lane_i == t, flag_mask(f, (1, BLK))))
    bnd_o[...] = jnp.sum(jnp.where(used, level, 0.0), axis=1, keepdims=True)


def body(
    observed,
    latent_noise,
    w_hidden,
    w_latent,
    w_frame,
    gate_bias,
    w_prior,
    w_emit,
    w_emit_hidden,
    block_source,
    inner_offset,
    resample_flags,
):
    D = lax.axis_size("dom")
    steps, Z, n = latent_noise.shape
    H = w_hidden.shape[1]
    X = w_emit.shape[0]
    G = 4 * H // CH
    V = pltpu.VMEM
    DMA = pltpu.SemaphoreType.DMA
    hidden, bound = pl.pallas_call(
        functools.partial(kernel, D),
        out_shape=(
            jax.ShapeDtypeStruct((H, n), BF16),
            jax.ShapeDtypeStruct((1, 1), F32),
        ),
        in_specs=[pl.BlockSpec(memory_space=pl.ANY)] * 12,
        out_specs=(
            pl.BlockSpec(memory_space=pl.ANY),
            pl.BlockSpec(memory_space=pltpu.VMEM),
        ),
        scratch_shapes=[
            V((CH, G, H), BF16),
            V((CH, G, Z + BLK), BF16),
            V((X, 4 * H), BF16),
            V((BLK, 4 * H), BF16),
            V((1, 4 * H), F32),
            V((2 * Z, H), BF16),
            V((X, Z), BF16),
            V((X, H), BF16),
            V((steps + 1, X), BF16),
            V((BLK, BLK), F32),
            V((steps, Z, n), F32),
            V(inner_offset.shape, jnp.int32),
            pltpu.SMEM(block_source.shape, jnp.int32),
            pltpu.SMEM(resample_flags.shape, jnp.int32),
            V((3, Z, n), F32),
            V((3, Z, n), F32),
            V((Z, n), BF16),
            V((Z, n), BF16),
            V((Z, n), BF16),
            V((Z, n), F32),
            V((Z, n), F32),
            V((Z, n), F32),
            V((CH, G, n), F32),
            V((G, 2 * n), F32),
            V((G, 2 * n), F32),
            V((H, n), BF16),
            V((H, n), BF16),
            V((H, n), BF16),
            V((H, n), BF16),
            V((H, n), BF16),
            V((H, n), BF16),
            V((H, 2 * n), BF16),
            V((H, 2 * n), BF16),
            V((H, 2 * n), BF16),
            V((H, 2 * n), BF16),
            V((H, n), BF16),
            V((1, BLK), F32),
            V((D, 1, BLK), F32),
            DMA((2, CH, 4)),
            DMA((16,)),
            DMA,
            DMA((2, 5)),
            DMA((2, 5)),
            DMA((D,)),
            DMA((D,)),
            pltpu.SemaphoreType.REGULAR((8,)),
        ],
        compiler_params=pltpu.CompilerParams(
            collective_id=0, has_side_effects=True, vmem_limit_bytes=60 * 2**20
        ),
        name="filter_steps",
    )(
        observed,
        latent_noise,
        w_hidden,
        w_latent,
        w_frame,
        gate_bias.reshape(1, -1),
        w_prior,
        w_emit,
        w_emit_hidden,
        block_source,
        inner_offset,
        resample_flags,
    )
    return hidden, bound.reshape(1)


def solution(mesh):
    in_specs = (
        P("seq", None),
        P(None, None, ("seq", "dom")),
        P(),
        P(),
        P(),
        P(),
        P(),
        P(),
        P(),
        P("seq", None),
        P("seq", None),
        P(),
    )
    out_specs = (P(None, ("seq", "dom")), P("seq"))
    return jax.shard_map(body, mesh=mesh, in_specs=in_specs, out_specs=out_specs, check_vma=False)
```

profile of v0, /device:TPU:4, one launch (start us, length us, event | category | flops | bytes accessed | tf_op | source)
XLA Modules:
  0.0 43.3 jit_solution(5604668830896072075)
XLA Ops:
  0.6 39.2 %filter_steps.1 = (bf16[1024,128]{1,0:T(8,128)(2,1)}, f32[1,1]{1,0:T(1,128)}) custom-call(bf16[5,88]{1,0:T(8,128)(2,1)} %obs_h.1, f32[4,128,128]{2,1,0:T(8,128)} %nz_h.1, bf16[4096,1024]{1,0:T(8,128)(2,1)} %wh_h.1, bf16[4096,128]{1,0:T(8,128)(2,1)} %wl_h.1, bf16[88,4096]{1,0:T(8,128)(2,1)} %wf_h.1, f32[1,4096]{1,0:T(1,128)} %bitcast.2, ...), custom_call_target="tpu_custom_call" | custom-call | tf_op jit(solution)/shard_map/filter_steps/pallas_call | solution.py:499
  39.8 1.7 %copy.16 = bf16[1024,128]{1,0:T(8,128)(2,1)} copy(bf16[1024,128]{1,0:T(8,128)(2,1)} %get-tuple-element.8) | data formatting | bytes 524288
where the time goes:
time: 43.4 us; the launch traced here: 43.3 us
  Pallas kernels  39.2 us (90%)
  between operations  2.41 us (6%)
  local copies, waits for them, and re-layouts  1.67 us (4%)
    pallas_call x1, Pallas kernels, body(): pl.pallas_call(functools.partial(kernel, D), out_shape=(jax.ShapeDtypeStr...  39.2 us
    unnamed x1, local copies, waits for them, and re-layouts  1.67 us

commit v1 on v0

--- a/solution.py
+++ b/solution.py
@@ -53,8 +53,9 @@
     bs_h,
     off_h,
     fl_h,
-    hid_o,
-    bnd_o,
+    h4,
+    lse_all,
+    used_o,
     wh,
     wlf,
     wf,
@@ -90,12 +91,9 @@
     c2,
     h3,
     c3,
-    h4,
     lse_row,
-    lse_all,
     wsem,
     lsem,
-    osem,
     ssem,
     rsem,
     as_sem,
@@ -109,10 +107,32 @@
     me = lax.axis_index("dom")
     right = lax.rem(me + 1, D)
     left = lax.rem(me + D - 1, D)
+    has_r, has_l = me < D - 1, me > 0
+
+    def signal(sem, dev, there):
+        @pl.when(there)
+        def _():
+            pl.semaphore_signal(sem, inc=1, device_id={"dom": dev}, device_id_type=MESH)
+
+    def partners(dist):
+        return (
+            (lax.rem(me + dist, D), me + dist < D),
+            (lax.rem(me + D - dist, D), me >= dist),
+        )
+
+    def count(dist):
+        return sum(jnp.where(there, 1, 0) for _, there in partners(dist))
 
     barrier = pltpu.get_barrier_semaphore()
-    for nb in (left, right):
-        pl.semaphore_signal(barrier, inc=1, device_id={"dom": nb}, device_id_type=MESH)
+    for dev, there in partners(1):
+        signal(barrier, dev, there)
+
+    def near_signal(i):
+        for dev, there in partners(2**i):
+            signal(near_sem.at[i], dev, there)
+
+    def near_wait(i):
+        pl.semaphore_wait(near_sem.at[i], count(2**i))
 
     small = []
 
@@ -122,13 +142,12 @@
         small.append(cp)
         return cp
 
-    cp_nz = [fetch(nz_h.at[t], nz.at[t]) for t in range(2)]
-    cp_bs = fetch(bs_h, bs)
-    cp_fl = fetch(fl_h, fl)
     cp_wf = fetch(wf_h, wf)
     cp_bias = fetch(bias_h, bias)
     cp_obs = fetch(obs_h, obs)
     cp_off = fetch(off_h, off)
+    cp_bs = fetch(bs_h, bs)
+    cp_fl = fetch(fl_h, fl)
 
     def weight_copies(c):
         res = []
@@ -147,42 +166,58 @@
         return res
 
     wcp = [weight_copies(c) for c in range(CH)]
-    for cp in wcp[0]:
-        cp.start()
+    for c in range(CH):
+        for cp in wcp[c]:
+            cp.start(priority=1)
     cp_wp = fetch(wp_h, wp)
-    cp_nz += [fetch(nz_h.at[t], nz.at[t]) for t in range(2, 4)]
+    cp_nz = fetch(nz_h, nz)
     cp_we = fetch(we_h, we)
     cp_weh = fetch(weh_h, weh)
-    for c in range(1, CH):
-        for cp in wcp[c]:
-            cp.start()
-
-    def send(k, src, to_right_dst, to_left_dst):
-        res = []
-        for side, (dst, dev) in enumerate(((to_right_dst, right), (to_left_dst, left))):
-            cp = pltpu.make_async_remote_copy(
-                src_ref=src,
-                dst_ref=dst,
-                send_sem=ssem.at[side, k],
-                recv_sem=rsem.at[side, k],
-                device_id={"dom": dev},
-                device_id_type=MESH,
-            )
-            cp.start()
-            res.append(cp)
-        return res
+
+    def link(side, k, src, dsts):
+        return pltpu.make_async_remote_copy(
+            src_ref=src,
+            dst_ref=dsts[side],
+            send_sem=ssem.at[side, k],
+            recv_sem=rsem.at[side, k],
+            device_id={"dom": (right, left)[side]},
+            device_id_type=MESH,
+        )
+
+    sent = {}
+
+    def send(k, src, *dsts):
+        sent[k] = (src, dsts)
+        for side, there in enumerate((has_r, has_l)):
+
+            @pl.when(there)
+            def _():
+                link(side, k, src, dsts).start()
+
+    def arrived(k):
+        for side, there in enumerate((has_l, has_r)):
+
+            @pl.when(there)
+            def _():
+                link(side, k, *sent[k]).wait_recv()
+
+    def all_sent():
+        for side, there in enumerate((has_r, has_l)):
+
+            @pl.when(there)
+            def _():
+                for k in sent:
+                    link(side, k, *sent[k]).wait_send()
+
+    pl.semaphore_wait(barrier, count(1))
+    send(0, nz_h.at[0], from_l.at[0], from_r.at[0])
+    send(1, nz_h.at[1], from_l.at[1], from_r.at[1])
+    near_signal(0)
 
     hz[...] = jnp.zeros_like(hz)
     cz[...] = jnp.zeros_like(cz)
     obs_pad[...] = jnp.zeros_like(obs_pad)
     tpose[X // 16 * 16 :, :] = jnp.zeros((BLK - X // 16 * 16, tpose.shape[1]), BF16)
-
-    cp_nz[0].wait()
-    cp_nz[1].wait()
-    pl.semaphore_wait(barrier, 2)
-    sent = []
-    for t in range(2):
-        sent += [send(t, nz.at[t], from_l.at[t], from_r.at[t])]
 
     cp_bs.wait()
     cp_fl.wait()
@@ -300,51 +335,32 @@
 
     lat_tail0 = jnp.concatenate([jnp.zeros((Z, BLK), BF16), tails[0]], axis=0)
 
-    def gates0(c):
+    for c in range(CH):
         for cp in wcp[c]:
             cp.wait()
-        return mm(wh[c], hz[...]) + mm(wlf[c], lat_tail0)
-
-    run_layer(gates0, elem_of(BLK, cz, h1, c1))
     cp_wp.wait()
-    mean0, std0 = moments(h1[...])
+    cp_nz.wait()
     cp_we.wait()
     cp_weh.wait()
-    lw0 = increment(0, (mean0 + std0 * nz[0]).astype(BF16), h1[...])
-
-    for c in range(CH // 2):
-        g1[c] = mm(wh[c], h1[...])
-
-    def near(i, dist):
-        for dev in (lax.rem(me + dist, D), lax.rem(me + D - dist, D)):
-            pl.semaphore_signal(
-                near_sem.at[i], inc=1, device_id={"dom": dev}, device_id_type=MESH
-            )
-
-    near(0, 1)
-
-    def arrived(k, bufs):
-        for cp in bufs[k]:
-            cp.wait_recv()
-
-    arrived(0, sent)
+    near_wait(0)
+    near_signal(1)
+    run_layer(lambda c: mm(wh[c], hz[...]) + mm(wlf[c], lat_tail0), elem_of(BLK, cz, h1, c1))
+    mean0, std0 = moments(h1[...])
+
+    arrived(0)
     n0 = pick(from_l[0], nz[0], from_r[0], x0_src)
     x0[...] = (mean0 + std0 * n0).astype(BF16)
-    arrived(1, sent)
+    arrived(1)
     x1[...] = pick(from_l[1], nz[1], from_r[1], s1)
-    for c in range(CH // 2, CH):
+    near_wait(1)
+    send(2, x0, x0_l, x0_r)
+    send(3, x1, x1_l, x1_r)
+    send(4, nz_h.at[2], from_l.at[2], from_r.at[2])
+    near_signal(2)
+    lw0 = increment(0, (mean0 + std0 * nz[0]).astype(BF16), h1[...])
+
+    for c in range(CH):
         g1[c] = mm(wh[c], h1[...])
-    sent += [send(2, x0, x0_l, x0_r)]
-    sent += [send(3, x1, x1_l, x1_r)]
-    cp_nz[2].wait()
-    cp_nz[3].wait()
-    sent += [send(4, nz.at[2], from_l.at[2], from_r.at[2])]
-    pl.semaphore_wait(near_sem.at[0], 2)
-    dist, count = 2, 1
-    waits = []
-    while dist < D // 2:
-        waits.append((count, dist))
-        dist, count = dist * 2, count + 1
 
     lat_c = mm(
         (mean0 + std0 * pick(from_l[0], nz[0], from_r[0], s0)).astype(BF16), hot_c0
@@ -355,9 +371,9 @@
     inc_c = increment(1, (mean_c + std_c * nz[1]).astype(BF16), hc[...])
     lw1 = jnp.where(flag_mask(f0, (1, BLK)), 0.0, lw0) + inc_c
 
-    for i, d in waits[:1]:
-        near(i, d)
-    arrived(2, sent)
+    near_wait(2)
+    near_signal(3)
+    arrived(2)
     x0s = (x0_l[...].astype(F32), x0[...].astype(F32), x0_r[...].astype(F32))
     lat_o = mm(pick(*x0s, hop_o).astype(BF16), hot_o0).astype(BF16)
     lat_l = mm(pick(*x0s, hop_l).astype(BF16), hot_s).astype(BF16)
@@ -381,12 +397,8 @@
         c2[rows, :] = s
 
     run_layer(gates1, elem1)
-    for i, d in waits[:1]:
-        pl.semaphore_wait(near_sem.at[i], 2)
-    for i, d in waits[1:2]:
-        near(i, d)
     m1, sd1 = moments(h2[...])
-    arrived(3, sent)
+    arrived(3)
     n1_o = gather3(x1[...], hot_o1)
     n1_l = gather3(pick(x1_l[...], x1[...], x1_r[...], k2), hot_r)
     lat1 = (m1 + sd1 * jnp.concatenate([n1_o, n1_l], axis=1)).astype(BF16)
@@ -397,12 +409,10 @@
     run_layer(
         lambda c: mm(wh[c], h2[...]) + mm(wlf[c], tail2), elem_of(2 * BLK, c2, h3, c3)
     )
-    for i, d in waits[1:2]:
-        pl.semaphore_wait(near_sem.at[i], 2)
-    for i, d in waits[2:3]:
-        near(i, d)
+    near_wait(3)
+    near_signal(4)
     m2, sd2 = moments(h3[...])
-    arrived(4, sent)
+    arrived(4)
     n2_l = gather3(pick(from_l[2], nz[2], from_r[2], k2), hot_q)
     lat2 = (m2 + sd2 * jnp.concatenate([nz[2], n2_l], axis=1)).astype(BF16)
     inc2 = increment(2, lat2[:, :BLK], h3[:, :BLK])
@@ -419,10 +429,6 @@
         h4[rows, :] = h
 
     run_layer(gates3, elem3)
-    out_cp = pltpu.make_async_copy(h4, hid_o, osem)
-    out_cp.start()
-    for i, d in waits[2:3]:
-        pl.semaphore_wait(near_sem.at[i], 2)
     m3, sd3 = moments(h4[...])
     lat3 = (m3 + sd3 * nz[3]).astype(BF16)
     lw3 = jnp.where(flag_mask(f2, (1, BLK)), 0.0, lw2) + increment(3, lat3, h4[...])
@@ -437,6 +443,11 @@
         row = jnp.where(lane_i == t, lse(lw), row)
     lse_row[...] = row
     lse_all[pl.ds(me, 1)] = row[None]
+    used = lane_i == steps - 1
+    for t, f in enumerate((f0, f1, f2)):
+        used = jnp.logical_or(used, jnp.logical_and(lane_i == t, flag_mask(f, (1, BLK))))
+    used_o[...] = jnp.where(used, 1.0, 0.0)
+    near_wait(4)
     pushes = []
     for d in range(1, D):
         dev = lax.rem(me + d, D)
@@ -450,10 +461,7 @@
         )
         cp.start()
         pushes.append(cp)
-    for two in sent:
-        for cp in two:
-            cp.wait_send()
-    out_cp.wait()
+    all_sent()
     for d in range(1, D):
         frm = lax.rem(me + d, D)
         pltpu.make_async_remote_copy(
@@ -466,13 +474,17 @@
         ).wait_recv()
     for cp in pushes:
         cp.wait_send()
+
+
+def finish(h_ref, lse_all, used, hid_o, bnd_o, sem):
+    out_cp = pltpu.make_async_copy(h_ref, hid_o, sem)
+    out_cp.start()
     every = lse_all[...]
     peak = jnp.max(every, axis=0)
-    level = peak + jnp.log(jnp.sum(jnp.exp(every - peak[None]), axis=0)) - math.log(D * BLK)
-    used = lane_i == steps - 1
-    for t, f in enumerate((f0, f1, f2)):
-        used = jnp.logical_or(used, jnp.logical_and(lane_i == t, flag_mask(f, (1, BLK))))
-    bnd_o[...] = jnp.sum(jnp.where(used, level, 0.0), axis=1, keepdims=True)
+    total = jnp.log(jnp.sum(jnp.exp(every - peak[None]), axis=0))
+    level = peak + total - math.log(every.shape[0] * BLK)
+    bnd_o[...] = jnp.sum(jnp.where(used[...] > 0, level, 0.0), axis=1, keepdims=True)
+    out_cp.wait()
 
 
 def body(
@@ -496,17 +508,32 @@
     G = 4 * H // CH
     V = pltpu.VMEM
     DMA = pltpu.SemaphoreType.DMA
-    hidden, bound = pl.pallas_call(
+    pinned = [
+        pltpu.with_memory_space_constraint(x, pltpu.HBM)
+        for x in (
+            observed,
+            latent_noise,
+            w_hidden,
+            w_latent,
+            w_frame,
+            gate_bias.reshape(1, -1),
+            w_prior,
+            w_emit,
+            w_emit_hidden,
+            block_source,
+            inner_offset,
+            resample_flags,
+        )
+    ]
+    last_hidden, lse_all, used = pl.pallas_call(
         functools.partial(kernel, D),
         out_shape=(
             jax.ShapeDtypeStruct((H, n), BF16),
-            jax.ShapeDtypeStruct((1, 1), F32),
+            jax.ShapeDtypeStruct((D, 1, BLK), F32),
+            jax.ShapeDtypeStruct((1, BLK), F32),
         ),
-        in_specs=[pl.BlockSpec(memory_space=pl.ANY)] * 12,
-        out_specs=(
-            pl.BlockSpec(memory_space=pl.ANY),
-            pl.BlockSpec(memory_space=pltpu.VMEM),
-        ),
+        in_specs=[pl.BlockSpec(memory_space=pltpu.HBM)] * 12,
+        out_specs=(pl.BlockSpec(memory_space=pltpu.VMEM),) * 3,
         scratch_shapes=[
             V((CH, G, H), BF16),
             V((CH, G, Z + BLK), BF16),
@@ -543,12 +570,9 @@
             V((H, 2 * n), BF16),
             V((H, 2 * n), BF16),
             V((H, 2 * n), BF16),
-            V((H, n), BF16),
             V((1, BLK), F32),
-            V((D, 1, BLK), F32),
             DMA((2, CH, 4)),
             DMA((16,)),
-            DMA,
             DMA((2, 5)),
             DMA((2, 5)),
             DMA((D,)),
@@ -556,23 +580,25 @@
             pltpu.SemaphoreType.REGULAR((8,)),
         ],
         compiler_params=pltpu.CompilerParams(
-            collective_id=0, has_side_effects=True, vmem_limit_bytes=60 * 2**20
+            collective_id=0, has_side_effects=True, vmem_limit_bytes=32 * 2**20
         ),
         name="filter_steps",
-    )(
-        observed,
-        latent_noise,
-        w_hidden,
-        w_latent,
-        w_frame,
-        gate_bias.reshape(1, -1),
-        w_prior,
-        w_emit,
-        w_emit_hidden,
-        block_source,
-        inner_offset,
-        resample_flags,
-    )
+    )(*pinned)
+    hidden, bound = pl.pallas_call(
+        finish,
+        out_shape=(
+            jax.ShapeDtypeStruct((H, n), BF16),
+            jax.ShapeDtypeStruct((1, 1), F32),
+        ),
+        in_specs=[pl.BlockSpec(memory_space=pltpu.VMEM)] * 3,
+        out_specs=(
+            pl.BlockSpec(memory_space=pl.ANY),
+            pl.BlockSpec(memory_space=pltpu.VMEM),
+        ),
+        scratch_shapes=[DMA],
+        compiler_params=pltpu.CompilerParams(vmem_limit_bytes=2 * 2**20),
+        name="finish",
+    )(last_hidden, lse_all, used)
     return hidden, bound.reshape(1)
 
 

time: 43.4 us -> 35.2 us (0.81)
  Pallas kernels: 39.2 us -> 34.3 us
  local copies, waits for them, and re-layouts: 1.67 us -> 0 us
  between operations: 2.41 us -> 0.8 us
    pallas_call x1, Pallas kernels: 39.2 us -> 33.1 us  [body(): pl.pallas_call(functools.partial(kernel, D), out_shape=(jax.ShapeDtypeStr...]
    unnamed x1 -> x0, local copies, waits for them, and re-layouts: 1.67 us -> none
    pallas_call x0 -> x1, Pallas kernels: none -> 1.23 us  [body(): pl.pallas_call(finish, out_shape=(jax.ShapeDtypeStruct((H, n), BF16), jax...]
where the time goes in v1:
time: 35.2 us; the launch traced here: 35.1 us
  Pallas kernels  34.3 us (97%)
  between operations  0.8 us (2%)
    pallas_call x1, Pallas kernels, body(): pl.pallas_call(functools.partial(kernel, D), out_shape=(jax.ShapeDtypeStr...  33.1 us
    pallas_call x1, Pallas kernels, body(): pl.pallas_call(finish, out_shape=(jax.ShapeDtypeStruct((H, n), BF16), jax...  1.23 us

profile of v1, /device:TPU:4, one launch (start us, length us, event | category | flops | bytes accessed | tf_op | source)
XLA Modules:
  0.0 35.1 jit_solution(8476571802195524383)
XLA Ops:
  0.6 33.1 %filter_steps.1 = (bf16[1024,128]{1,0:T(8,128)(2,1)S(1)}, f32[32,1,128]{2,1,0:T(1,128)S(1)}, f32[1,128]{1,0:T(1,128)S(1)}) custom-call(bf16[5,88]{1,0:T(8,128)(2,1)} %obs_h.1, f32[4,128,128]{2,1,0:T(8,128)} %nz_h.1, bf16[4096,1024]{1,0:T(8,128)(2,1)} %wh_h.1, bf16[4096,128]{1,0:T(8,128)(2,1)} %wl_h.1, bf16[88,4096]{1,0:T(8,128)(2,1)} %wf_h.1, ...), custom_call_target="tpu_custom_call" | custom-call | tf_op jit(solution)/shard_map/filter_steps/pallas_call | solution.py:528
  33.8 1.2 %finish.1 = (bf16[1024,128]{1,0:T(8,128)(2,1)}, f32[1,1]{1,0:T(1,128)}) custom-call(bf16[1024,128]{1,0:T(8,128)(2,1)S(1)} %get-tuple-element.7.h_ref, f32[32,1,128]{2,1,0:T(1,128)S(1)} %get-tuple-element.8.lse_all, f32[1,128]{1,0:T(1,128)S(1)} %get-tuple-element.9.used), custom_call_target="tpu_custom_call" | custom-call | tf_op jit(solution)/shard_map/finish/pallas_call | solution.py:587

commit v2 on v1

--- a/solution.py
+++ b/solution.py
@@ -81,12 +81,13 @@
     g1,
     ga,
     gb,
+    gc,
+    gd,
     hz,
     cz,
     h1,
     c1,
     hc,
-    cc,
     h2,
     c2,
     h3,
@@ -100,7 +101,7 @@
     ar_sem,
     near_sem,
 ):
-    H = wh.shape[2]
+    H = wh.shape[3]
     Z = we.shape[1]
     X = we.shape[0]
     HC = H // CH
@@ -142,6 +143,7 @@
         small.append(cp)
         return cp
 
+    cp_n01 = fetch(nz_h.at[pl.ds(0, 2)], nz.at[pl.ds(0, 2)])
     cp_wf = fetch(wf_h, wf)
     cp_bias = fetch(bias_h, bias)
     cp_obs = fetch(obs_h, obs)
@@ -149,28 +151,18 @@
     cp_bs = fetch(bs_h, bs)
     cp_fl = fetch(fl_h, fl)
 
-    def weight_copies(c):
-        res = []
-        for g in range(4):
-            rows = pl.ds(g * H + c * HC, HC)
-            res.append(
-                pltpu.make_async_copy(
-                    wh_h.at[rows, :], wh.at[c, pl.ds(g * HC, HC), :], wsem.at[0, c, g]
-                )
-            )
-            res.append(
-                pltpu.make_async_copy(
-                    wl_h.at[rows, :], wlf.at[c, pl.ds(g * HC, HC), pl.ds(0, Z)], wsem.at[1, c, g]
-                )
-            )
-        return res
-
-    wcp = [weight_copies(c) for c in range(CH)]
-    for c in range(CH):
-        for cp in wcp[c]:
+    wcp = [
+        (
+            pltpu.make_async_copy(wh_h.at[:, c], wh.at[c], wsem.at[0, c]),
+            pltpu.make_async_copy(wl_h.at[:, c], wlf.at[c, :, :, pl.ds(0, Z)], wsem.at[1, c]),
+        )
+        for c in range(CH)
+    ]
+    for pair in wcp:
+        for cp in pair:
             cp.start(priority=1)
     cp_wp = fetch(wp_h, wp)
-    cp_nz = fetch(nz_h, nz)
+    cp_n23 = fetch(nz_h.at[pl.ds(2, 2)], nz.at[pl.ds(2, 2)])
     cp_we = fetch(we_h, we)
     cp_weh = fetch(weh_h, weh)
 
@@ -178,7 +170,7 @@
         return pltpu.make_async_remote_copy(
             src_ref=src,
             dst_ref=dsts[side],
-            send_sem=ssem.at[side, k],
+            send_sem=ssem.at[side, max(k - 2, 0)],
             recv_sem=rsem.at[side, k],
             device_id={"dom": (right, left)[side]},
             device_id_type=MESH,
@@ -206,12 +198,16 @@
 
             @pl.when(there)
             def _():
-                for k in sent:
+                noise = pl.ds(0, 3)
+                link(side, 0, nz_h.at[noise], (from_l.at[noise], from_r.at[noise])).wait_send()
+                for k in (3, 4):
                     link(side, k, *sent[k]).wait_send()
 
     pl.semaphore_wait(barrier, count(1))
-    send(0, nz_h.at[0], from_l.at[0], from_r.at[0])
-    send(1, nz_h.at[1], from_l.at[1], from_r.at[1])
+    cp_n01.wait()
+    for t in range(2):
+        send(t, nz.at[t], from_l.at[t], from_r.at[t])
+    send(2, nz_h.at[2], from_l.at[2], from_r.at[2])
     near_signal(0)
 
     hz[...] = jnp.zeros_like(hz)
@@ -301,7 +297,7 @@
         for g in range(4):
             for i in range(0, HC, BLK):
                 rows = g * H + c * HC + i
-                wlf[c, g * HC + i : g * HC + i + BLK, Z : Z + BLK] = jnp.transpose(
+                wlf[c, g, i : i + BLK, Z : Z + BLK] = jnp.transpose(
                     tpose[:, rows : rows + BLK]
                 )
 
@@ -335,45 +331,55 @@
 
     lat_tail0 = jnp.concatenate([jnp.zeros((Z, BLK), BF16), tails[0]], axis=0)
 
-    for c in range(CH):
-        for cp in wcp[c]:
-            cp.wait()
+    def w_h(c):
+        return wh[c].reshape(4 * HC, H)
+
+    def w_lf(c):
+        return wlf[c].reshape(4 * HC, Z + BLK)
+
+    def gates0(c):
+        if c % (CH // 2) == 0:
+            for pair in wcp[c : c + CH // 2]:
+                for cp in pair:
+                    cp.wait()
+        return mm(w_h(c), hz[...]) + mm(w_lf(c), lat_tail0)
+
+    run_layer(gates0, elem_of(BLK, cz, h1, c1))
     cp_wp.wait()
-    cp_nz.wait()
+    cp_n23.wait()
     cp_we.wait()
     cp_weh.wait()
-    near_wait(0)
-    near_signal(1)
-    run_layer(lambda c: mm(wh[c], hz[...]) + mm(wlf[c], lat_tail0), elem_of(BLK, cz, h1, c1))
     mean0, std0 = moments(h1[...])
 
     arrived(0)
     n0 = pick(from_l[0], nz[0], from_r[0], x0_src)
     x0[...] = (mean0 + std0 * n0).astype(BF16)
+    near_wait(0)
+    send(3, x0, x0_l, x0_r)
     arrived(1)
     x1[...] = pick(from_l[1], nz[1], from_r[1], s1)
-    near_wait(1)
-    send(2, x0, x0_l, x0_r)
-    send(3, x1, x1_l, x1_r)
-    send(4, nz_h.at[2], from_l.at[2], from_r.at[2])
-    near_signal(2)
+    near_signal(1)
+    send(4, x1, x1_l, x1_r)
     lw0 = increment(0, (mean0 + std0 * nz[0]).astype(BF16), h1[...])
-
-    for c in range(CH):
-        g1[c] = mm(wh[c], h1[...])
 
     lat_c = mm(
         (mean0 + std0 * pick(from_l[0], nz[0], from_r[0], s0)).astype(BF16), hot_c0
     ).astype(BF16)
     tail_c = jnp.concatenate([lat_c, tails[1]], axis=0)
-    run_layer(lambda c: g1[c] + mm(wlf[c], tail_c), elem_of(BLK, c1, hc, None))
+
+    def gates_c(c):
+        g = mm(w_h(c), h1[...])
+        g1[c] = g
+        return g + mm(w_lf(c), tail_c)
+
+    run_layer(gates_c, elem_of(BLK, c1, hc, None))
+    near_wait(1)
+    arrived(3)
+    near_signal(2)
     mean_c, std_c = moments(hc[...])
     inc_c = increment(1, (mean_c + std_c * nz[1]).astype(BF16), hc[...])
     lw1 = jnp.where(flag_mask(f0, (1, BLK)), 0.0, lw0) + inc_c
 
-    near_wait(2)
-    near_signal(3)
-    arrived(2)
     x0s = (x0_l[...].astype(F32), x0[...].astype(F32), x0_r[...].astype(F32))
     lat_o = mm(pick(*x0s, hop_o).astype(BF16), hot_o0).astype(BF16)
     lat_l = mm(pick(*x0s, hop_l).astype(BF16), hot_s).astype(BF16)
@@ -387,7 +393,7 @@
 
     def gates1(c):
         g = g1[c]
-        return jnp.concatenate([g, g], axis=1) + mm(wlf[c], tail_ol)
+        return jnp.concatenate([g, g], axis=1) + mm(w_lf(c), tail_ol)
 
     def elem1(c, buf):
         rows = slice(c * HC, (c + 1) * HC)
@@ -398,7 +404,13 @@
 
     run_layer(gates1, elem1)
     m1, sd1 = moments(h2[...])
-    arrived(3)
+    early = (gc, gd)
+    for c in range(2):
+        early[c][...] = mm(w_h(c), h2[...])
+    near_wait(2)
+    arrived(4)
+    arrived(2)
+    near_signal(3)
     n1_o = gather3(x1[...], hot_o1)
     n1_l = gather3(pick(x1_l[...], x1[...], x1_r[...], k2), hot_r)
     lat1 = (m1 + sd1 * jnp.concatenate([n1_o, n1_l], axis=1)).astype(BF16)
@@ -406,13 +418,15 @@
     tail2 = jnp.concatenate(
         [lat1, jnp.concatenate([tails[2], tails[2]], axis=1)], axis=0
     )
-    run_layer(
-        lambda c: mm(wh[c], h2[...]) + mm(wlf[c], tail2), elem_of(2 * BLK, c2, h3, c3)
-    )
+
+    def gates2(c):
+        part = early[c][...] if c < 2 else mm(w_h(c), h2[...])
+        return part + mm(w_lf(c), tail2)
+
+    run_layer(gates2, elem_of(2 * BLK, c2, h3, c3))
     near_wait(3)
     near_signal(4)
     m2, sd2 = moments(h3[...])
-    arrived(4)
     n2_l = gather3(pick(from_l[2], nz[2], from_r[2], k2), hot_q)
     lat2 = (m2 + sd2 * jnp.concatenate([nz[2], n2_l], axis=1)).astype(BF16)
     inc2 = increment(2, lat2[:, :BLK], h3[:, :BLK])
@@ -421,7 +435,7 @@
     tail3 = jnp.concatenate([lat2[:, BLK:], tails[3]], axis=0)
 
     def gates3(c):
-        return mm(wh[c], h3[:, BLK:]) + mm(wlf[c], tail3)
+        return mm(w_h(c), h3[:, BLK:]) + mm(w_lf(c), tail3)
 
     def elem3(c, buf):
         rows = slice(c * HC, (c + 1) * HC)
@@ -448,32 +462,27 @@
         used = jnp.logical_or(used, jnp.logical_and(lane_i == t, flag_mask(f, (1, BLK))))
     used_o[...] = jnp.where(used, 1.0, 0.0)
     near_wait(4)
-    pushes = []
     for d in range(1, D):
-        dev = lax.rem(me + d, D)
-        cp = pltpu.make_async_remote_copy(
+        pltpu.make_async_remote_copy(
             src_ref=lse_row,
             dst_ref=lse_all.at[me],
-            send_sem=as_sem.at[d],
-            recv_sem=ar_sem.at[me],
-            device_id={"dom": dev},
+            send_sem=as_sem,
+            recv_sem=ar_sem,
+            device_id={"dom": lax.rem(me + d, D)},
             device_id_type=MESH,
-        )
-        cp.start()
-        pushes.append(cp)
+        ).start()
     all_sent()
-    for d in range(1, D):
-        frm = lax.rem(me + d, D)
-        pltpu.make_async_remote_copy(
-            src_ref=lse_row,
-            dst_ref=lse_all.at[frm],
-            send_sem=as_sem.at[d],
-            recv_sem=ar_sem.at[frm],
-            device_id={"dom": frm},
-            device_id_type=MESH,
-        ).wait_recv()
-    for cp in pushes:
-        cp.wait_send()
+    others = lse_all.at[pl.ds(0, D - 1)]
+    every = pltpu.make_async_remote_copy(
+        src_ref=others,
+        dst_ref=others,
+        send_sem=as_sem,
+        recv_sem=ar_sem,
+        device_id={"dom": right},
+        device_id_type=MESH,
+    )
+    every.wait_recv()
+    every.wait_send()
 
 
 def finish(h_ref, lse_all, used, hid_o, bnd_o, sem):
@@ -513,8 +522,8 @@
         for x in (
             observed,
             latent_noise,
-            w_hidden,
-            w_latent,
+            w_hidden.reshape(4, CH, H // CH, H),
+            w_latent.reshape(4, CH, H // CH, Z),
             w_frame,
             gate_bias.reshape(1, -1),
             w_prior,
@@ -535,8 +544,8 @@
         in_specs=[pl.BlockSpec(memory_space=pltpu.HBM)] * 12,
         out_specs=(pl.BlockSpec(memory_space=pltpu.VMEM),) * 3,
         scratch_shapes=[
-            V((CH, G, H), BF16),
-            V((CH, G, Z + BLK), BF16),
+            V((CH, 4, H // CH, H), BF16),
+            V((CH, 4, H // CH, Z + BLK), BF16),
             V((X, 4 * H), BF16),
             V((BLK, 4 * H), BF16),
             V((1, 4 * H), F32),
@@ -560,7 +569,8 @@
             V((CH, G, n), F32),
             V((G, 2 * n), F32),
             V((G, 2 * n), F32),
-            V((H, n), BF16),
+            V((G, 2 * n), F32),
+            V((G, 2 * n), F32),
             V((H, n), BF16),
             V((H, n), BF16),
             V((H, n), BF16),
@@ -571,13 +581,13 @@
             V((H, 2 * n), BF16),
             V((H, 2 * n), BF16),
             V((1, BLK), F32),
-            DMA((2, CH, 4)),
-            DMA((16,)),
+            DMA((2, CH)),
+            DMA((11,)),
+            DMA((2, 3)),
             DMA((2, 5)),
-            DMA((2, 5)),
-            DMA((D,)),
-            DMA((D,)),
-            pltpu.SemaphoreType.REGULAR((8,)),
+            DMA,
+            DMA,
+            pltpu.SemaphoreType.REGULAR((5,)),
         ],
         compiler_params=pltpu.CompilerParams(
             collective_id=0, has_side_effects=True, vmem_limit_bytes=32 * 2**20

time: 35.2 us -> 34.4 us (0.977)
  Pallas kernels: 34.3 us -> 33.5 us
    pallas_call x1, Pallas kernels: 33.1 us -> 32.3 us  [body(): pl.pallas_call(functools.partial(kernel, D), out_shape=(jax.ShapeDtypeStr...]
where the time goes in v2:
time: 34.4 us; the launch traced here: 34.3 us
  Pallas kernels  33.5 us (97%)
  between operations  0.8 us (2%)
    pallas_call x1, Pallas kernels, body(): pl.pallas_call(functools.partial(kernel, D), out_shape=(jax.ShapeDtypeStr...  32.3 us
    pallas_call x1, Pallas kernels, body(): pl.pallas_call(finish, out_shape=(jax.ShapeDtypeStruct((H, n), BF16), jax...  1.23 us

profile of v2, /device:TPU:4, one launch (start us, length us, event | category | flops | bytes accessed | tf_op | source)
XLA Modules:
  0.0 34.3 jit_solution(6728579075414504867)
XLA Ops:
  0.6 32.3 %filter_steps.1 = (bf16[1024,128]{1,0:T(8,128)(2,1)S(1)}, f32[32,1,128]{2,1,0:T(1,128)S(1)}, f32[1,128]{1,0:T(1,128)S(1)}) custom-call(bf16[5,88]{1,0:T(8,128)(2,1)} %obs_h.1, f32[4,128,128]{2,1,0:T(8,128)} %nz_h.1, bf16[4,4,256,1024]{3,2,1,0:T(8,128)(2,1)} %bitcast.4, bf16[4,4,256,128]{3,2,1,0:T(8,128)(2,1)} %bitcast.5, bf16[88,4096]{1,0:T(8,128)(2,1)} %wf_h.1, ...), custom_call_target="tpu_custom_call" | custom-call | tf_op jit(solution)/shard_map/filter_steps/pallas_call | solution.py:537
  32.9 1.2 %finish.1 = (bf16[1024,128]{1,0:T(8,128)(2,1)}, f32[1,1]{1,0:T(1,128)}) custom-call(bf16[1024,128]{1,0:T(8,128)(2,1)S(1)} %get-tuple-element.7.h_ref, f32[32,1,128]{2,1,0:T(1,128)S(1)} %get-tuple-element.8.lse_all, f32[1,128]{1,0:T(1,128)S(1)} %get-tuple-element.9.used), custom_call_target="tpu_custom_call" | custom-call | tf_op jit(solution)/shard_map/finish/pallas_call | solution.py:597

commit v3 on v2

--- a/solution.py
+++ b/solution.py
@@ -12,7 +12,7 @@
 F32 = jnp.float32
 BF16 = jnp.bfloat16
 MESH = pl.DeviceIdType.MESH
-CH = 4
+CH = 8
 
 
 def mm(a, b):
@@ -70,19 +70,14 @@
     off,
     bs,
     fl,
-    from_l,
-    from_r,
+    rx,
     x0,
-    x0_l,
-    x0_r,
-    x1,
-    x1_l,
-    x1_r,
+    x0_far,
+    x1_far,
     g1,
     ga,
     gb,
     gc,
-    gd,
     hz,
     cz,
     h1,
@@ -108,7 +103,6 @@
     me = lax.axis_index("dom")
     right = lax.rem(me + 1, D)
     left = lax.rem(me + D - 1, D)
-    has_r, has_l = me < D - 1, me > 0
 
     def signal(sem, dev, there):
         @pl.when(there)
@@ -166,49 +160,64 @@
     cp_we = fetch(we_h, we)
     cp_weh = fetch(weh_h, weh)
 
-    def link(side, k, src, dsts):
+    def link(side, k):
+        src, dst = (
+            (nz.at[0], rx.at[side, 0]),
+            (nz.at[1], rx.at[side, 1]),
+            (nz_h.at[2], rx.at[side, 2]),
+            (x0.at[side], x0_far.at[side]),
+            (rx.at[side, 1], x1_far.at[side]),
+        )[k]
         return pltpu.make_async_remote_copy(
             src_ref=src,
-            dst_ref=dsts[side],
+            dst_ref=dst,
             send_sem=ssem.at[side, max(k - 2, 0)],
             recv_sem=rsem.at[side, k],
-            device_id={"dom": (right, left)[side]},
+            device_id={"dom": lax.rem(me + 1 - 2 * side + D, D)},
             device_id_type=MESH,
         )
 
-    sent = {}
-
-    def send(k, src, *dsts):
-        sent[k] = (src, dsts)
-        for side, there in enumerate((has_r, has_l)):
-
-            @pl.when(there)
+    def within(place):
+        return jnp.logical_and(place >= 0, place < D)
+
+    def step_of(side):
+        return 1 - 2 * side
+
+    def sends(side, k):
+        ahead = within(me + step_of(side))
+        return ahead if k < 3 else jnp.logical_and(ahead, within(me - step_of(side)))
+
+    def send(side, k):
+        @pl.when(sends(side, k))
+        def _():
+            link(side, k).start()
+
+    def arrived(k, sides=(0, 1)):
+        for side in sides:
+
+            @pl.when(within(me - (1 if k < 3 else 2) * step_of(side)))
             def _():
-                link(side, k, src, dsts).start()
-
-    def arrived(k):
-        for side, there in enumerate((has_l, has_r)):
-
-            @pl.when(there)
-            def _():
-                link(side, k, *sent[k]).wait_recv()
+                link(side, k).wait_recv()
 
     def all_sent():
-        for side, there in enumerate((has_r, has_l)):
-
-            @pl.when(there)
+        for side in range(2):
+
+            @pl.when(sends(side, 0))
             def _():
                 noise = pl.ds(0, 3)
-                link(side, 0, nz_h.at[noise], (from_l.at[noise], from_r.at[noise])).wait_send()
-                for k in (3, 4):
-                    link(side, k, *sent[k]).wait_send()
-
-    pl.semaphore_wait(barrier, count(1))
-    cp_n01.wait()
-    for t in range(2):
-        send(t, nz.at[t], from_l.at[t], from_r.at[t])
-    send(2, nz_h.at[2], from_l.at[2], from_r.at[2])
-    near_signal(0)
+                pltpu.make_async_remote_copy(
+                    src_ref=nz_h.at[noise],
+                    dst_ref=rx.at[side, noise],
+                    send_sem=ssem.at[side, 0],
+                    recv_sem=rsem.at[side, 0],
+                    device_id={"dom": lax.rem(me + step_of(side) + D, D)},
+                    device_id_type=MESH,
+                ).wait_send()
+
+            @pl.when(sends(side, 3))
+            def _():
+                link(side, 3).wait_send()
+                link(side, 4).wait_send()
 
     hz[...] = jnp.zeros_like(hz)
     cz[...] = jnp.zeros_like(cz)
@@ -255,20 +264,28 @@
     k1 = src(1, k2, f1)
     s1 = src(1, me, f1)
     s0 = src(0, me, f0)
-    both = jnp.logical_and(f0, f1)
+    o0 = src(0, s1, f0)
+    k0 = src(0, k1, f0)
     hot_q = onehot(offs(2, me, f2))
     hot_r = onehot(comp(offs(1, k2, f1), hot_q))
     hot_s = onehot(comp(offs(0, k1, f0), hot_r))
     hot_o1 = onehot(offs(1, me, f1))
     hot_o0 = onehot(comp(offs(0, s1, f0), hot_o1))
     hot_c0 = onehot(offs(0, me, f0))
-    x0_src = jnp.where(f0, s0, s1)
-    hop_o = jnp.where(both, s1, me)
-    hop_l = jnp.where(f2, k2, hop_o)
-
-    def pick(a, b, c, k):
-        d = jnp.broadcast_to(k - me, a.shape)
-        return jnp.where(d < 0, a, jnp.where(d > 0, c, b))
+    def pick(t, k):
+        d = jnp.broadcast_to(k - me, (Z, BLK))
+        out = jnp.where(d < 0, rx[0, t], jnp.where(d > 0, rx[1, t], nz[t]))
+        if t != 1:
+            return out
+        return jnp.where(d == -2, x1_far[0], jnp.where(d == 2, x1_far[1], out))
+
+    def latent_0(k, hot, far=True):
+        lat = mean0 + std0 * pick(0, k)
+        if far:
+            d = jnp.broadcast_to(k - me, (Z, BLK))
+            lat = jnp.where(d == -2, x0_far[0].astype(F32), lat)
+            lat = jnp.where(d == 2, x0_far[1].astype(F32), lat)
+        return mm(lat.astype(BF16), hot).astype(BF16)
 
     def gather3(x, hot):
         hi, mid, lo = split3(x)
@@ -301,9 +318,17 @@
                     tpose[:, rows : rows + BLK]
                 )
 
-    def run_layer(gates, elem):
+    pl.semaphore_wait(barrier, count(1))
+    cp_n01.wait()
+    for t in range(3):
+        for side in range(2):
+            send(side, t)
+    near_signal(0)
+
+    def run_layer(gates, elem, hooks={}):
         bufs = (ga, gb)
         for c in range(CH):
+            hooks.get(c, lambda: None)()
             val = gates(c)
             bufs[c % 2][:, : val.shape[1]] = val
             if c:
@@ -321,8 +346,7 @@
         return elem
 
     def moments(h):
-        p = mm(wp[...], h)
-        return p[:Z], jnp.exp(0.5 * jnp.tanh(p[Z:]))
+        return mm(wp[:Z, :], h), jnp.exp(0.5 * jnp.tanh(mm(wp[Z:, :], h)))
 
     def increment(t, lat, h):
         pred = mm(we[...], lat) + mm(weh[...], h)
@@ -337,52 +361,66 @@
     def w_lf(c):
         return wlf[c].reshape(4 * HC, Z + BLK)
 
-    def gates0(c):
-        if c % (CH // 2) == 0:
-            for pair in wcp[c : c + CH // 2]:
-                for cp in pair:
-                    cp.wait()
-        return mm(w_h(c), hz[...]) + mm(w_lf(c), lat_tail0)
-
-    run_layer(gates0, elem_of(BLK, cz, h1, c1))
-    cp_wp.wait()
-    cp_n23.wait()
-    cp_we.wait()
-    cp_weh.wait()
+    def weights_here(c):
+        for pair in wcp[c : c + 2]:
+            for cp in pair:
+                cp.wait()
+
+    def third():
+        weights_here(4)
+        near_wait(0)
+        near_signal(1)
+
+    def fourth():
+        weights_here(6)
+        cp_wp.wait()
+        cp_n23.wait()
+        cp_we.wait()
+        cp_weh.wait()
+
+    run_layer(
+        lambda c: mm(w_h(c), hz[...]) + mm(w_lf(c), lat_tail0),
+        elem_of(BLK, cz, h1, c1),
+        {0: lambda: weights_here(0), 2: lambda: weights_here(2), 4: third, 6: fourth},
+    )
     mean0, std0 = moments(h1[...])
 
-    arrived(0)
-    n0 = pick(from_l[0], nz[0], from_r[0], x0_src)
-    x0[...] = (mean0 + std0 * n0).astype(BF16)
-    near_wait(0)
-    send(3, x0, x0_l, x0_r)
-    arrived(1)
-    x1[...] = pick(from_l[1], nz[1], from_r[1], s1)
-    near_signal(1)
-    send(4, x1, x1_l, x1_r)
+    def relay_0(side):
+        arrived(0, (side,))
+        x0[side] = (mean0 + std0 * rx[side, 0]).astype(BF16)
+        send(side, 3)
+
+    first = jnp.where(lax.rem(me, 4) == 0, 1, 0)
+    relay_0(first)
+    for c in range(2):
+        g1[c] = mm(w_h(c), h1[...])
+    relay_0(1 - first)
+    near_wait(1)
+    near_signal(2)
+    lat_c = latent_0(s0, hot_c0, False)
+    tail_c = jnp.concatenate([lat_c, tails[1]], axis=0)
     lw0 = increment(0, (mean0 + std0 * nz[0]).astype(BF16), h1[...])
 
-    lat_c = mm(
-        (mean0 + std0 * pick(from_l[0], nz[0], from_r[0], s0)).astype(BF16), hot_c0
-    ).astype(BF16)
-    tail_c = jnp.concatenate([lat_c, tails[1]], axis=0)
-
     def gates_c(c):
-        g = mm(w_h(c), h1[...])
-        g1[c] = g
-        return g + mm(w_lf(c), tail_c)
-
-    run_layer(gates_c, elem_of(BLK, c1, hc, None))
-    near_wait(1)
+        if c > 1:
+            g1[c] = mm(w_h(c), h1[...])
+        return g1[c] + mm(w_lf(c), tail_c)
+
+    def relay_1():
+        arrived(1)
+        send(0, 4)
+        send(1, 4)
+
+    run_layer(gates_c, elem_of(BLK, c1, hc, None), {4: relay_1})
+    near_wait(2)
     arrived(3)
-    near_signal(2)
+    near_signal(3)
     mean_c, std_c = moments(hc[...])
     inc_c = increment(1, (mean_c + std_c * nz[1]).astype(BF16), hc[...])
     lw1 = jnp.where(flag_mask(f0, (1, BLK)), 0.0, lw0) + inc_c
 
-    x0s = (x0_l[...].astype(F32), x0[...].astype(F32), x0_r[...].astype(F32))
-    lat_o = mm(pick(*x0s, hop_o).astype(BF16), hot_o0).astype(BF16)
-    lat_l = mm(pick(*x0s, hop_l).astype(BF16), hot_s).astype(BF16)
+    lat_o = latent_0(o0, hot_o0)
+    lat_l = latent_0(k0, hot_s)
     tail_ol = jnp.concatenate(
         [
             jnp.concatenate([lat_o, lat_l], axis=1),
@@ -404,15 +442,18 @@
 
     run_layer(gates1, elem1)
     m1, sd1 = moments(h2[...])
-    early = (gc, gd)
-    for c in range(2):
-        early[c][...] = mm(w_h(c), h2[...])
-    near_wait(2)
+    early = CH // 2
+    late = early + 2
+    for c in range(early):
+        gc[c] = mm(w_h(c), h2[...])
+    near_wait(3)
     arrived(4)
     arrived(2)
-    near_signal(3)
-    n1_o = gather3(x1[...], hot_o1)
-    n1_l = gather3(pick(x1_l[...], x1[...], x1_r[...], k2), hot_r)
+    near_signal(4)
+    n1_o = gather3(pick(1, s1), hot_o1)
+    n1_l = gather3(pick(1, k1), hot_r)
+    for c in range(early, late):
+        gc[c] = mm(w_h(c), h2[...])
     lat1 = (m1 + sd1 * jnp.concatenate([n1_o, n1_l], axis=1)).astype(BF16)
 
     tail2 = jnp.concatenate(
@@ -420,22 +461,20 @@
     )
 
     def gates2(c):
-        part = early[c][...] if c < 2 else mm(w_h(c), h2[...])
+        part = gc[c] if c < late else mm(w_h(c), h2[...])
         return part + mm(w_lf(c), tail2)
 
     run_layer(gates2, elem_of(2 * BLK, c2, h3, c3))
-    near_wait(3)
-    near_signal(4)
     m2, sd2 = moments(h3[...])
-    n2_l = gather3(pick(from_l[2], nz[2], from_r[2], k2), hot_q)
+    for c in range(2):
+        g1[c] = mm(w_h(c), h3[:, BLK:])
+    n2_l = gather3(pick(2, k2), hot_q)
     lat2 = (m2 + sd2 * jnp.concatenate([nz[2], n2_l], axis=1)).astype(BF16)
-    inc2 = increment(2, lat2[:, :BLK], h3[:, :BLK])
-    lw2 = jnp.where(flag_mask(f1, (1, BLK)), 0.0, lw1) + inc2
-
     tail3 = jnp.concatenate([lat2[:, BLK:], tails[3]], axis=0)
 
     def gates3(c):
-        return mm(w_h(c), h3[:, BLK:]) + mm(w_lf(c), tail3)
+        part = g1[c] if c < 2 else mm(w_h(c), h3[:, BLK:])
+        return part + mm(w_lf(c), tail3)
 
     def elem3(c, buf):
         rows = slice(c * HC, (c + 1) * HC)
@@ -443,6 +482,8 @@
         h4[rows, :] = h
 
     run_layer(gates3, elem3)
+    inc2 = increment(2, lat2[:, :BLK], h3[:, :BLK])
+    lw2 = jnp.where(flag_mask(f1, (1, BLK)), 0.0, lw1) + inc2
     m3, sd3 = moments(h4[...])
     lat3 = (m3 + sd3 * nz[3]).astype(BF16)
     lw3 = jnp.where(flag_mask(f2, (1, BLK)), 0.0, lw2) + increment(3, lat3, h4[...])
@@ -558,19 +599,14 @@
             V(inner_offset.shape, jnp.int32),
             pltpu.SMEM(block_source.shape, jnp.int32),
             pltpu.SMEM(resample_flags.shape, jnp.int32),
-            V((3, Z, n), F32),
-            V((3, Z, n), F32),
-            V((Z, n), BF16),
-            V((Z, n), BF16),
-            V((Z, n), BF16),
-            V((Z, n), F32),
-            V((Z, n), F32),
-            V((Z, n), F32),
+            V((2, 3, Z, n), F32),
+            V((2, Z, n), BF16),
+            V((2, Z, n), BF16),
+            V((2, Z, n), F32),
             V((CH, G, n), F32),
             V((G, 2 * n), F32),
             V((G, 2 * n), F32),
-            V((G, 2 * n), F32),
-            V((G, 2 * n), F32),
+            V((CH // 2 + 2, G, 2 * n), F32),
             V((H, n), BF16),
             V((H, n), BF16),
             V((H, n), BF16),

time: 34.4 us -> 33.8 us (0.983)
  Pallas kernels: 33.5 us -> 32.9 us
    pallas_call x1, Pallas kernels: 32.3 us -> 31.7 us  [body(): pl.pallas_call(functools.partial(kernel, D), out_shape=(jax.ShapeDtypeStr...]
where the time goes in v3:
time: 33.8 us; the launch traced here: 33.7 us
  Pallas kernels  32.9 us (97%)
  between operations  0.8 us (2%)
    pallas_call x1, Pallas kernels, body(): pl.pallas_call(functools.partial(kernel, D), out_shape=(jax.ShapeDtypeStr...  31.7 us
    pallas_call x1, Pallas kernels, body(): pl.pallas_call(finish, out_shape=(jax.ShapeDtypeStruct((H, n), BF16), jax...  1.23 us

profile of v3, /device:TPU:4, one launch (start us, length us, event | category | flops | bytes accessed | tf_op | source)
XLA Modules:
  0.0 33.7 jit_solution(14503069213315768681)
XLA Ops:
  0.6 31.7 %filter_steps.1 = (bf16[1024,128]{1,0:T(8,128)(2,1)S(1)}, f32[32,1,128]{2,1,0:T(1,128)S(1)}, f32[1,128]{1,0:T(1,128)S(1)}) custom-call(bf16[5,88]{1,0:T(8,128)(2,1)} %obs_h.1, f32[4,128,128]{2,1,0:T(8,128)} %nz_h.1, bf16[4,8,128,1024]{3,2,1,0:T(8,128)(2,1)} %bitcast.4, bf16[4,8,128,128]{3,2,1,0:T(8,128)(2,1)} %bitcast.5, bf16[88,4096]{1,0:T(8,128)(2,1)} %wf_h.1, ...), custom_call_target="tpu_custom_call" | custom-call | tf_op jit(solution)/shard_map/filter_steps/pallas_call | solution.py:578
  32.3 1.2 %finish.1 = (bf16[1024,128]{1,0:T(8,128)(2,1)}, f32[1,1]{1,0:T(1,128)}) custom-call(bf16[1024,128]{1,0:T(8,128)(2,1)S(1)} %get-tuple-element.7.h_ref, f32[32,1,128]{2,1,0:T(1,128)S(1)} %get-tuple-element.8.lse_all, f32[1,128]{1,0:T(1,128)S(1)} %get-tuple-element.9.used), custom_call_target="tpu_custom_call" | custom-call | tf_op jit(solution)/shard_map/finish/pallas_call | solution.py:633

commit v4 on v3

--- a/solution.py
+++ b/solution.py
@@ -152,9 +152,12 @@
         )
         for c in range(CH)
     ]
-    for pair in wcp:
-        for cp in pair:
-            cp.start(priority=1)
+    def start_weights(c, n):
+        for pair in wcp[c : c + n]:
+            for cp in pair:
+                cp.start(priority=1)
+
+    start_weights(0, 2)
     cp_wp = fetch(wp_h, wp)
     cp_n23 = fetch(nz_h.at[pl.ds(2, 2)], nz.at[pl.ds(2, 2)])
     cp_we = fetch(we_h, we)
@@ -224,6 +227,7 @@
     obs_pad[...] = jnp.zeros_like(obs_pad)
     tpose[X // 16 * 16 :, :] = jnp.zeros((BLK - X // 16 * 16, tpose.shape[1]), BF16)
 
+    start_weights(2, 6)
     cp_bs.wait()
     cp_fl.wait()
     cp_off.wait()
@@ -355,33 +359,47 @@
 
     lat_tail0 = jnp.concatenate([jnp.zeros((Z, BLK), BF16), tails[0]], axis=0)
 
-    def w_h(c):
-        return wh[c].reshape(4 * HC, H)
-
-    def w_lf(c):
-        return wlf[c].reshape(4 * HC, Z + BLK)
-
-    def weights_here(c):
-        for pair in wcp[c : c + 2]:
+    def halves(c, first, tail=None):
+        out = []
+        for g in (0, 2):
+            rows = slice(g * HC, (g + 2) * HC)
+            val = first(g, rows)
+            if tail is not None:
+                val = val + mm(wlf[c, g : g + 2].reshape(2 * HC, Z + BLK), tail)
+            out.append(val)
+        return jnp.concatenate(out, axis=0)
+
+    def product(c, state, tail=None):
+        def first(g, rows):
+            return mm(wh[c, g : g + 2].reshape(2 * HC, H), state)
+
+        return halves(c, first, tail)
+
+    def with_tail(c, ref, tail, wide=False):
+        def first(g, rows):
+            part = ref[c, rows, :]
+            return jnp.concatenate([part, part], axis=1) if wide else part
+
+        return halves(c, first, tail)
+
+    def weights_here(c, n):
+        for pair in wcp[c : c + n]:
             for cp in pair:
                 cp.wait()
 
     def third():
-        weights_here(4)
+        weights_here(4, 4)
         near_wait(0)
         near_signal(1)
-
-    def fourth():
-        weights_here(6)
         cp_wp.wait()
         cp_n23.wait()
         cp_we.wait()
         cp_weh.wait()
 
     run_layer(
-        lambda c: mm(w_h(c), hz[...]) + mm(w_lf(c), lat_tail0),
+        lambda c: product(c, hz[...], lat_tail0),
         elem_of(BLK, cz, h1, c1),
-        {0: lambda: weights_here(0), 2: lambda: weights_here(2), 4: third, 6: fourth},
+        {0: lambda: weights_here(0, 2), 2: lambda: weights_here(2, 2), 4: third},
     )
     mean0, std0 = moments(h1[...])
 
@@ -392,9 +410,19 @@
 
     first = jnp.where(lax.rem(me, 4) == 0, 1, 0)
     relay_0(first)
+    inner = jnp.logical_or(lax.rem(me, 4) == 1, lax.rem(me, 4) == 2)
+
+    @pl.when(inner)
+    def _():
+        relay_0(1 - first)
+
     for c in range(2):
-        g1[c] = mm(w_h(c), h1[...])
-    relay_0(1 - first)
+        g1[c] = product(c, h1[...])
+
+    @pl.when(jnp.logical_not(inner))
+    def _():
+        relay_0(1 - first)
+
     near_wait(1)
     near_signal(2)
     lat_c = latent_0(s0, hot_c0, False)
@@ -403,8 +431,8 @@
 
     def gates_c(c):
         if c > 1:
-            g1[c] = mm(w_h(c), h1[...])
-        return g1[c] + mm(w_lf(c), tail_c)
+            g1[c] = product(c, h1[...])
+        return with_tail(c, g1, tail_c)
 
     def relay_1():
         arrived(1)
@@ -430,8 +458,7 @@
     )
 
     def gates1(c):
-        g = g1[c]
-        return jnp.concatenate([g, g], axis=1) + mm(w_lf(c), tail_ol)
+        return with_tail(c, g1, tail_ol, True)
 
     def elem1(c, buf):
         rows = slice(c * HC, (c + 1) * HC)
@@ -442,10 +469,9 @@
 
     run_layer(gates1, elem1)
     m1, sd1 = moments(h2[...])
-    early = CH // 2
-    late = early + 2
+    early, late = 2, 4
     for c in range(early):
-        gc[c] = mm(w_h(c), h2[...])
+        gc[c] = product(c, h2[...])
     near_wait(3)
     arrived(4)
     arrived(2)
@@ -453,7 +479,7 @@
     n1_o = gather3(pick(1, s1), hot_o1)
     n1_l = gather3(pick(1, k1), hot_r)
     for c in range(early, late):
-        gc[c] = mm(w_h(c), h2[...])
+        gc[c] = product(c, h2[...])
     lat1 = (m1 + sd1 * jnp.concatenate([n1_o, n1_l], axis=1)).astype(BF16)
 
     tail2 = jnp.concatenate(
@@ -461,20 +487,22 @@
     )
 
     def gates2(c):
-        part = gc[c] if c < late else mm(w_h(c), h2[...])
-        return part + mm(w_lf(c), tail2)
+        if c < late:
+            return with_tail(c, gc, tail2)
+        return product(c, h2[...], tail2)
 
     run_layer(gates2, elem_of(2 * BLK, c2, h3, c3))
     m2, sd2 = moments(h3[...])
     for c in range(2):
-        g1[c] = mm(w_h(c), h3[:, BLK:])
+        g1[c] = product(c, h3[:, BLK:])
     n2_l = gather3(pick(2, k2), hot_q)
     lat2 = (m2 + sd2 * jnp.concatenate([nz[2], n2_l], axis=1)).astype(BF16)
     tail3 = jnp.concatenate([lat2[:, BLK:], tails[3]], axis=0)
 
     def gates3(c):
-        part = g1[c] if c < 2 else mm(w_h(c), h3[:, BLK:])
-        return part + mm(w_lf(c), tail3)
+        if c < 2:
+            return with_tail(c, g1, tail3)
+        return product(c, h3[:, BLK:], tail3)
 
     def elem3(c, buf):
         rows = slice(c * HC, (c + 1) * HC)
@@ -526,15 +554,18 @@
     every.wait_send()
 
 
-def finish(h_ref, lse_all, used, hid_o, bnd_o, sem):
-    out_cp = pltpu.make_async_copy(h_ref, hid_o, sem)
+def finish(h_ref, lse_all, used, hid_o, bnd_o, bnd, sem):
+    out_cp = pltpu.make_async_copy(h_ref, hid_o, sem.at[0])
     out_cp.start()
     every = lse_all[...]
     peak = jnp.max(every, axis=0)
     total = jnp.log(jnp.sum(jnp.exp(every - peak[None]), axis=0))
     level = peak + total - math.log(every.shape[0] * BLK)
-    bnd_o[...] = jnp.sum(jnp.where(used[...] > 0, level, 0.0), axis=1, keepdims=True)
+    bnd[...] = jnp.sum(jnp.where(used[...] > 0, level, 0.0), axis=1, keepdims=True)
+    bnd_cp = pltpu.make_async_copy(bnd, bnd_o, sem.at[1])
+    bnd_cp.start()
     out_cp.wait()
+    bnd_cp.wait()
 
 
 def body(
@@ -637,11 +668,8 @@
             jax.ShapeDtypeStruct((1, 1), F32),
         ),
         in_specs=[pl.BlockSpec(memory_space=pltpu.VMEM)] * 3,
-        out_specs=(
-            pl.BlockSpec(memory_space=pl.ANY),
-            pl.BlockSpec(memory_space=pltpu.VMEM),
-        ),
-        scratch_shapes=[DMA],
+        out_specs=(pl.BlockSpec(memory_space=pl.ANY),) * 2,
+        scratch_shapes=[V((1, 1), F32), DMA((2,))],
         compiler_params=pltpu.CompilerParams(vmem_limit_bytes=2 * 2**20),
         name="finish",
     )(last_hidden, lse_all, used)

time: 33.8 us -> 33.2 us (0.982)
  Pallas kernels: 32.9 us -> 32.3 us
    pallas_call x1, Pallas kernels: 1.23 us -> 0.73 us  [body(): pl.pallas_call(finish, out_shape=(jax.ShapeDtypeStruct((H, n), BF16), jax...]
where the time goes in v4:
time: 33.2 us; the launch traced here: 33.1 us
  Pallas kernels  32.3 us (97%)
  between operations  0.8 us (2%)
    pallas_call x1, Pallas kernels, body(): pl.pallas_call(functools.partial(kernel, D), out_shape=(jax.ShapeDtypeStr...  31.6 us
    pallas_call x1, Pallas kernels, body(): pl.pallas_call(finish, out_shape=(jax.ShapeDtypeStruct((H, n), BF16), jax...  0.73 us

profile of v4, /device:TPU:4, one launch (start us, length us, event | category | flops | bytes accessed | tf_op | source)
XLA Modules:
  0.0 33.1 jit_solution(14200400147801880631)
XLA Ops:
  0.6 31.6 %filter_steps.1 = (bf16[1024,128]{1,0:T(8,128)(2,1)S(1)}, f32[32,1,128]{2,1,0:T(1,128)S(1)}, f32[1,128]{1,0:T(1,128)S(1)}) custom-call(bf16[5,88]{1,0:T(8,128)(2,1)} %obs_h.1, f32[4,128,128]{2,1,0:T(8,128)} %nz_h.1, bf16[4,8,128,1024]{3,2,1,0:T(8,128)(2,1)} %bitcast.4, bf16[4,8,128,128]{3,2,1,0:T(8,128)(2,1)} %bitcast.5, bf16[88,4096]{1,0:T(8,128)(2,1)} %wf_h.1, ...), custom_call_target="tpu_custom_call" | custom-call | tf_op jit(solution)/shard_map/filter_steps/pallas_call | solution.py:609
  32.2 0.7 %finish.1 = (bf16[1024,128]{1,0:T(8,128)(2,1)}, f32[1,1]{1,0:T(1,128)}) custom-call(bf16[1024,128]{1,0:T(8,128)(2,1)S(1)} %get-tuple-element.7.h_ref, f32[32,1,128]{2,1,0:T(1,128)S(1)} %get-tuple-element.8.lse_all, f32[1,128]{1,0:T(1,128)S(1)} %get-tuple-element.9.used), custom_call_target="tpu_custom_call" | custom-call | tf_op jit(solution)/shard_map/finish/pallas_call | solution.py:664

commit v5 on v4

--- a/solution.py
+++ b/solution.py
@@ -443,9 +443,6 @@
     near_wait(2)
     arrived(3)
     near_signal(3)
-    mean_c, std_c = moments(hc[...])
-    inc_c = increment(1, (mean_c + std_c * nz[1]).astype(BF16), hc[...])
-    lw1 = jnp.where(flag_mask(f0, (1, BLK)), 0.0, lw0) + inc_c
 
     lat_o = latent_0(o0, hot_o0)
     lat_l = latent_0(k0, hot_s)
@@ -472,6 +469,9 @@
     early, late = 2, 4
     for c in range(early):
         gc[c] = product(c, h2[...])
+    mean_c, std_c = moments(hc[...])
+    inc_c = increment(1, (mean_c + std_c * nz[1]).astype(BF16), hc[...])
+    lw1 = jnp.where(flag_mask(f0, (1, BLK)), 0.0, lw0) + inc_c
     near_wait(3)
     arrived(4)
     arrived(2)

time: 33.2 us -> 33.1 us (level)
  no operation moved by 1% of the time
where the time goes in v5:
time: 33.1 us; the launch traced here: 33 us
  Pallas kernels  32.2 us (97%)
  between operations  0.8 us (2%)
    pallas_call x1, Pallas kernels, body(): pl.pallas_call(functools.partial(kernel, D), out_shape=(jax.ShapeDtypeStr...  31.5 us
    pallas_call x1, Pallas kernels, body(): pl.pallas_call(finish, out_shape=(jax.ShapeDtypeStruct((H, n), BF16), jax...  0.73 us

profile of v5, /device:TPU:4, one launch (start us, length us, event | category | flops | bytes accessed | tf_op | source)
XLA Modules:
  0.0 33.0 jit_solution(9402072916463987810)
XLA Ops:
  0.6 31.5 %filter_steps.1 = (bf16[1024,128]{1,0:T(8,128)(2,1)S(1)}, f32[32,1,128]{2,1,0:T(1,128)S(1)}, f32[1,128]{1,0:T(1,128)S(1)}) custom-call(bf16[5,88]{1,0:T(8,128)(2,1)} %obs_h.1, f32[4,128,128]{2,1,0:T(8,128)} %nz_h.1, bf16[4,8,128,1024]{3,2,1,0:T(8,128)(2,1)} %bitcast.4, bf16[4,8,128,128]{3,2,1,0:T(8,128)(2,1)} %bitcast.5, bf16[88,4096]{1,0:T(8,128)(2,1)} %wf_h.1, ...), custom_call_target="tpu_custom_call" | custom-call | tf_op jit(solution)/shard_map/filter_steps/pallas_call | solution.py:609
  32.1 0.7 %finish.1 = (bf16[1024,128]{1,0:T(8,128)(2,1)}, f32[1,1]{1,0:T(1,128)}) custom-call(bf16[1024,128]{1,0:T(8,128)(2,1)S(1)} %get-tuple-element.7.h_ref, f32[32,1,128]{2,1,0:T(1,128)S(1)} %get-tuple-element.8.lse_all, f32[1,128]{1,0:T(1,128)S(1)} %get-tuple-element.9.used), custom_call_target="tpu_custom_call" | custom-call | tf_op jit(solution)/shard_map/finish/pallas_call | solution.py:664
